TPU v7x, 32 devices: a whole 2x2x4 slice. The times are simulated.
32 devices in a mesh: replica: 2 (over x), fsdp: 16 (over z, y, core).
Axes of the slice: x: 2, y: 2, z: 4, core: 2. Of those that a mesh axis runs over, the one named last changes fastest.
Arguments:
- tokens: bfloat16 [16384, 768], P(('replica', 'fsdp')), may hold values from -6 to 6
- cotangent: bfloat16 [16384, 768], P(('replica', 'fsdp')), may hold values from -6 to 6
- qkv_weight: bfloat16 [768, 2304], P('fsdp'), may hold values from -0.21875 to 0.21875
- qkv_bias: bfloat16 [2304], P('fsdp'), may hold values from -3 to 3
- proj_weight: bfloat16 [768, 768], P('fsdp'), may hold values from -1.75 to 1.75
- proj_bias: bfloat16 [768], P('fsdp'), may hold values from -3 to 3
- attn_gain: bfloat16 [768], P('fsdp'), may hold values from 0.5 to 1.5
- attn_shift: bfloat16 [768], P('fsdp'), may hold values from -3 to 3
- inner_weight: bfloat16 [768, 3072], P('fsdp'), may hold values from -0.21875 to 0.21875
- inner_bias: bfloat16 [3072], P('fsdp'), may hold values from -3 to 3
- outer_weight: bfloat16 [3072, 768], P('fsdp'), may hold values from -0.21875 to 0.21875
- outer_bias: bfloat16 [768], P('fsdp'), may hold values from -3 to 3
- ffn_gain: bfloat16 [768], P('fsdp'), may hold values from 0.5 to 1.5
- ffn_shift: bfloat16 [768], P('fsdp'), may hold values from -3 to 3
- random_dirs: bfloat16 [12, 64, 256], replicated, may hold values from -5 to 5
- seq_lengths: int32 [2, 16, 4], P('replica', 'fsdp'), may hold values from 1 to 256, 448 in all within a row
- deal_order: int32 [2, 16], P('replica'), may hold values from 0 to 15, each once within a row
Outputs:
- layer_out: bfloat16 [16384, 768], P(('replica', 'fsdp'))
- tokens_grad: bfloat16 [16384, 768], P(('replica', 'fsdp'))
- qkv_weight_grad: float32 [768, 2304], P('fsdp')
- qkv_bias_grad: float32 [2304], P('fsdp')
- proj_weight_grad: float32 [768, 768], P('fsdp')
- proj_bias_grad: float32 [768], P('fsdp')
- attn_gain_grad: float32 [768], P('fsdp')
- attn_shift_grad: float32 [768], P('fsdp')
- inner_weight_grad: float32 [768, 3072], P('fsdp')
- inner_bias_grad: float32 [3072], P('fsdp')
- outer_weight_grad: float32 [3072, 768], P('fsdp')
- outer_bias_grad: float32 [768], P('fsdp')
- ffn_gain_grad: float32 [768], P('fsdp')
- ffn_shift_grad: float32 [768], P('fsdp')
Inputs may be any that keep to these rules, and one draw needn't show every extreme that they name: `seq_lengths`: the 4 sequences of each dealt buffer lie one after another in its first 448 rows, the longest of each exactly 256 rows; the last 64 rows are padding. `deal_order`: each row is a permutation of the 16 buffers of one replica group.
All inputs are finite; a program needn't handle non-finite values.
Results may differ from a plain program's by a relative error of at most 0.03.
Values may be sent and summed in bfloat16 or wider, within the bound.
A program may use at most 128 MiB of HBM per device.

v0:
```python
from functools import partial
import jax
import jax.numpy as jnp
from jax import lax
from jax.sharding import PartitionSpec as P

EPSILON = 1e-06


def layer_norm(summed, gain_vec, shift_vec):
    centered = summed - jnp.mean(summed, -1, keepdims=True)
    inv_std = lax.rsqrt(jnp.mean(centered * centered, -1, keepdims=True) + EPSILON)
    return centered * inv_std * gain_vec + shift_vec


def matrix_product(left, right):
    return jnp.dot(left, right, preferred_element_type=jnp.float32)


def rows_product(left, right):
    return lax.dot_general(
        left, right, (((0,), (0,)), ((), ())), preferred_element_type=jnp.float32
    )


def back_product(left, right):
    return lax.dot_general(
        left, right, (((1,), (1,)), ((), ())), preferred_element_type=jnp.float32
    )


def feature_map(scaled, directions):
    project = jnp.einsum("rhd,hdm->rhm", scaled, directions, preferred_element_type=jnp.float32)
    widened = scaled.astype(jnp.float32)
    return jnp.exp(project - 0.5 * jnp.sum(widened * widened, -1, keepdims=True))


def feature_back(dfeature, feature, scaled, directions):
    dexponent = dfeature * feature
    dproject = dexponent.astype(jnp.bfloat16)
    dscaled = jnp.einsum("rhm,hdm->rhd", dproject, directions, preferred_element_type=jnp.float32)
    return dscaled - scaled.astype(jnp.float32) * jnp.sum(dexponent, -1, keepdims=True)


def unpack(gathered):
    return tuple(
        (tensor.astype(jnp.float32) if tensor.ndim == 1 else tensor for tensor in gathered)
    )


def column_sum(values_low):
    return jnp.sum(values_low.astype(jnp.float32), axis=0)


def body(
    tokens,
    cotangent,
    qkv_weight,
    qkv_bias,
    proj_weight,
    proj_bias,
    attn_gain,
    attn_shift,
    inner_weight,
    inner_bias,
    outer_weight,
    outer_bias,
    ffn_gain,
    ffn_shift,
    random_dirs,
    seq_lengths,
    deal_order,
):
    groups = lax.axis_size("fsdp")
    row_count, model_width = tokens.shape
    piece_rows = row_count // groups
    deal_row = deal_order[0]
    send_tokens = jnp.take(tokens.reshape(groups, piece_rows, model_width), deal_row, axis=0)
    send_grads = jnp.take(cotangent.reshape(groups, piece_rows, model_width), deal_row, axis=0)
    arrived_x, arrived_g = (
        lax.all_to_all(send_tokens, "fsdp", split_axis=0, concat_axis=0, tiled=True),
        lax.all_to_all(send_grads, "fsdp", split_axis=0, concat_axis=0, tiled=True),
    )
    token_low = arrived_x.reshape(row_count, model_width)
    upstream = arrived_g.reshape(row_count, model_width).astype(jnp.float32)
    gathered = (
        lax.all_gather(qkv_weight, "fsdp", axis=0, tiled=True),
        lax.all_gather(qkv_bias, "fsdp", axis=0, tiled=True),
        lax.all_gather(proj_weight, "fsdp", axis=0, tiled=True),
        lax.all_gather(proj_bias, "fsdp", axis=0, tiled=True),
        lax.all_gather(attn_gain, "fsdp", axis=0, tiled=True),
        lax.all_gather(attn_shift, "fsdp", axis=0, tiled=True),
        lax.all_gather(inner_weight, "fsdp", axis=0, tiled=True),
        lax.all_gather(inner_bias, "fsdp", axis=0, tiled=True),
        lax.all_gather(outer_weight, "fsdp", axis=0, tiled=True),
        lax.all_gather(outer_bias, "fsdp", axis=0, tiled=True),
        lax.all_gather(ffn_gain, "fsdp", axis=0, tiled=True),
        lax.all_gather(ffn_shift, "fsdp", axis=0, tiled=True),
    )
    (
        weight_qkv,
        bias_qkv,
        weight_proj,
        bias_proj,
        gain_attn,
        shift_attn,
        weight_inner,
        bias_inner,
        weight_outer,
        bias_outer,
        gain_ffn,
        shift_ffn,
    ) = unpack(gathered)
    lengths_here = seq_lengths[0, 0]
    seq_ends = jnp.cumsum(lengths_here)
    slot_count = lengths_here.shape[0] + 1
    position = lax.iota(jnp.int32, row_count)
    segment = jnp.sum((position[:, None] >= seq_ends[None, :]).astype(jnp.int32), axis=1)
    select_low = (segment[:, None] == lax.iota(jnp.int32, slot_count)[None, :]).astype(jnp.bfloat16)
    valid_rows = (segment < slot_count - 1).astype(jnp.float32)[:, None]
    head_count, head_dim = (random_dirs.shape[0], random_dirs.shape[1])
    feature_scale = head_dim ** (-0.25)
    qkv_act = matrix_product(token_low, weight_qkv) + bias_qkv
    query_act, key_act, value_act = jnp.split(qkv_act, 3, axis=1)
    query_low = (
        (query_act * feature_scale).astype(jnp.bfloat16).reshape(row_count, head_count, head_dim)
    )
    key_low = (
        (key_act * feature_scale).astype(jnp.bfloat16).reshape(row_count, head_count, head_dim)
    )
    value_low = value_act.astype(jnp.bfloat16).reshape(row_count, head_count, head_dim)
    query_feat = feature_map(query_low, random_dirs)
    key_feat = feature_map(key_low, random_dirs)
    qfeat_low = query_feat.astype(jnp.bfloat16)
    kfeat_low = key_feat.astype(jnp.bfloat16)
    masked_keys = select_low[:, :, None, None] * kfeat_low[:, None]
    masked_query = select_low[:, :, None, None] * qfeat_low[:, None]
    kv_state = jnp.einsum(
        "rshm,rhe->shme", masked_keys, value_low, preferred_element_type=jnp.float32
    ).astype(jnp.bfloat16)
    key_total = jnp.einsum(
        "rs,rhm->shm", select_low, kfeat_low, preferred_element_type=jnp.float32
    ).astype(jnp.bfloat16)
    numerator = jnp.einsum(
        "rshm,shme->rhe", masked_query, kv_state, preferred_element_type=jnp.float32
    )
    denominator = jnp.einsum(
        "rshm,shm->rh", masked_query, key_total, preferred_element_type=jnp.float32
    )
    context_low = (
        (numerator / denominator[:, :, None]).reshape(row_count, model_width).astype(jnp.bfloat16)
    )
    attn_out = matrix_product(context_low, weight_proj) + bias_proj
    hidden, first_pull = jax.vjp(
        layer_norm, token_low.astype(jnp.float32) + attn_out, gain_attn, shift_attn
    )
    hidden_low = hidden.astype(jnp.bfloat16)
    inner_act = matrix_product(hidden_low, weight_inner) + bias_inner
    gelu_act, gelu_pull = jax.vjp(partial(jax.nn.gelu, approximate=False), inner_act)
    gelu_low = gelu_act.astype(jnp.bfloat16)
    outer_act = matrix_product(gelu_low, weight_outer) + bias_outer
    normed_out, second_pull = jax.vjp(layer_norm, hidden + outer_act, gain_ffn, shift_ffn)
    result = normed_out * valid_rows
    regathered = (
        lax.all_gather(qkv_weight, "fsdp", axis=0, tiled=True),
        lax.all_gather(qkv_bias, "fsdp", axis=0, tiled=True),
        lax.all_gather(proj_weight, "fsdp", axis=0, tiled=True),
        lax.all_gather(proj_bias, "fsdp", axis=0, tiled=True),
        lax.all_gather(attn_gain, "fsdp", axis=0, tiled=True),
        lax.all_gather(attn_shift, "fsdp", axis=0, tiled=True),
        lax.all_gather(inner_weight, "fsdp", axis=0, tiled=True),
        lax.all_gather(inner_bias, "fsdp", axis=0, tiled=True),
        lax.all_gather(outer_weight, "fsdp", axis=0, tiled=True),
        lax.all_gather(outer_bias, "fsdp", axis=0, tiled=True),
        lax.all_gather(ffn_gain, "fsdp", axis=0, tiled=True),
        lax.all_gather(ffn_shift, "fsdp", axis=0, tiled=True),
    )
    back_weights = unpack(regathered)
    back_qkv = back_weights[0]
    back_proj = back_weights[2]
    back_inner = back_weights[6]
    back_outer = back_weights[8]
    dsecond, grad_gain_ffn, grad_shift_ffn = second_pull(upstream * valid_rows)
    douter_low = dsecond.astype(jnp.bfloat16)
    grad_bias_outer = column_sum(douter_low)
    grad_weight_outer = rows_product(gelu_low, douter_low)
    dinner_low = gelu_pull(back_product(douter_low, back_outer))[0].astype(jnp.bfloat16)
    grad_bias_inner = column_sum(dinner_low)
    grad_weight_inner = rows_product(hidden_low, dinner_low)
    dhidden = dsecond + back_product(dinner_low, back_inner)
    dfirst, grad_gain_attn, grad_shift_attn = first_pull(dhidden)
    dattn_low = dfirst.astype(jnp.bfloat16)
    grad_bias_proj = column_sum(dattn_low)
    grad_weight_proj = rows_product(context_low, dattn_low)
    dcontext = back_product(dattn_low, back_proj).reshape(row_count, head_count, head_dim)
    dnumer_low = (dcontext / denominator[:, :, None]).astype(jnp.bfloat16)
    ddenom_low = (-jnp.sum(dcontext * numerator, -1) / jnp.square(denominator)).astype(jnp.bfloat16)
    masked_dnumer = select_low[:, :, None, None] * dnumer_low[:, None]
    key_rows = jnp.einsum("rs,shm->rhm", select_low, key_total, preferred_element_type=jnp.float32)
    dqfeat = jnp.einsum(
        "rshe,shme->rhm", masked_dnumer, kv_state, preferred_element_type=jnp.float32
    )
    dqfeat = dqfeat + ddenom_low.astype(jnp.float32)[:, :, None] * key_rows
    dstate_low = jnp.einsum(
        "rshm,rhe->shme", masked_query, dnumer_low, preferred_element_type=jnp.float32
    ).astype(jnp.bfloat16)
    dtotal_low = jnp.einsum(
        "rshm,rh->shm", masked_query, ddenom_low, preferred_element_type=jnp.float32
    ).astype(jnp.bfloat16)
    masked_values = select_low[:, :, None, None] * value_low[:, None]
    dkfeat = jnp.einsum(
        "rshe,shme->rhm", masked_values, dstate_low, preferred_element_type=jnp.float32
    )
    dkfeat = dkfeat + jnp.einsum(
        "rs,shm->rhm", select_low, dtotal_low, preferred_element_type=jnp.float32
    )
    dvalues = jnp.einsum(
        "rshm,shme->rhe", masked_keys, dstate_low, preferred_element_type=jnp.float32
    )
    dquery = feature_back(dqfeat, query_feat, query_low, random_dirs) * feature_scale
    dkeys = feature_back(dkfeat, key_feat, key_low, random_dirs) * feature_scale
    dqkv_low = jnp.concatenate(
        [
            dquery.reshape(row_count, model_width),
            dkeys.reshape(row_count, model_width),
            dvalues.reshape(row_count, model_width),
        ],
        axis=1,
    ).astype(jnp.bfloat16)
    grad_bias_qkv = column_sum(dqkv_low)
    grad_weight_qkv = rows_product(token_low, dqkv_low)
    dtokens = dfirst + back_product(dqkv_low, back_qkv)
    group_sums = (
        lax.psum_scatter(grad_weight_qkv, "fsdp", scatter_dimension=0, tiled=True),
        lax.psum_scatter(grad_bias_qkv, "fsdp", scatter_dimension=0, tiled=True),
        lax.psum_scatter(grad_weight_proj, "fsdp", scatter_dimension=0, tiled=True),
        lax.psum_scatter(grad_bias_proj, "fsdp", scatter_dimension=0, tiled=True),
        lax.psum_scatter(grad_gain_attn, "fsdp", scatter_dimension=0, tiled=True),
        lax.psum_scatter(grad_shift_attn, "fsdp", scatter_dimension=0, tiled=True),
        lax.psum_scatter(grad_weight_inner, "fsdp", scatter_dimension=0, tiled=True),
        lax.psum_scatter(grad_bias_inner, "fsdp", scatter_dimension=0, tiled=True),
        lax.psum_scatter(grad_weight_outer, "fsdp", scatter_dimension=0, tiled=True),
        lax.psum_scatter(grad_bias_outer, "fsdp", scatter_dimension=0, tiled=True),
        lax.psum_scatter(grad_gain_ffn, "fsdp", scatter_dimension=0, tiled=True),
        lax.psum_scatter(grad_shift_ffn, "fsdp", scatter_dimension=0, tiled=True),
    )
    (
        sum_wqkv,
        sum_bqkv,
        sum_wproj,
        sum_bproj,
        sum_gattn,
        sum_sattn,
        sum_winner,
        sum_binner,
        sum_wouter,
        sum_bouter,
        sum_gffn,
        sum_sffn,
    ) = group_sums
    totals = lax.psum(
        (
            sum_wqkv,
            sum_bqkv,
            sum_wproj,
            sum_bproj,
            sum_gattn,
            sum_sattn,
            sum_winner,
            sum_binner,
            sum_wouter,
            sum_bouter,
            sum_gffn,
            sum_sffn,
        ),
        "replica",
    )
    out_rows = result.astype(jnp.bfloat16).reshape(groups, piece_rows, model_width)
    grad_rows = dtokens.astype(jnp.bfloat16).reshape(groups, piece_rows, model_width)
    back_out, back_grad = (
        lax.all_to_all(out_rows, "fsdp", split_axis=0, concat_axis=0, tiled=True),
        lax.all_to_all(grad_rows, "fsdp", split_axis=0, concat_axis=0, tiled=True),
    )
    inverse = jnp.zeros((groups,), jnp.int32).at[deal_row].set(lax.iota(jnp.int32, groups))
    layer_out = jnp.take(back_out, inverse, axis=0).reshape(row_count, model_width)
    tokens_grad = jnp.take(back_grad, inverse, axis=0).reshape(row_count, model_width)
    return (
        layer_out,
        tokens_grad,
        totals[0],
        totals[1],
        totals[2],
        totals[3],
        totals[4],
        totals[5],
        totals[6],
        totals[7],
        totals[8],
        totals[9],
        totals[10],
        totals[11],
    )


def solution(mesh):
    return jax.shard_map(
        body,
        mesh=mesh,
        in_specs=(
            P(("replica", "fsdp"), None),
            P(("replica", "fsdp"), None),
            P("fsdp", None),
            P("fsdp"),
            P("fsdp", None),
            P("fsdp"),
            P("fsdp"),
            P("fsdp"),
            P("fsdp", None),
            P("fsdp"),
            P("fsdp", None),
            P("fsdp"),
            P("fsdp"),
            P("fsdp"),
            P(),
            P("replica", "fsdp", None),
            P("replica", None),
        ),
        out_specs=(
            P(("replica", "fsdp"), None),
            P(("replica", "fsdp"), None),
            P("fsdp", None),
            P("fsdp"),
            P("fsdp", None),
            P("fsdp"),
            P("fsdp"),
            P("fsdp"),
            P("fsdp", None),
            P("fsdp"),
            P("fsdp", None),
            P("fsdp"),
            P("fsdp"),
            P("fsdp"),
        ),
        check_vma=False,
    )
```

profile of v0, /device:TPU:0, one launch (start us, length us, event | category | flops | bytes accessed | tf_op | source)
XLA Modules:
  0.0 745.2 jit_solution(5544804439539207280)
XLA Ops:
  10.8 1.8 gather_fusion
  14.0 7.4 all-to-all-start
  26.5 71.3 %all-reduce.19 = (bf16[2304]{0:T(1024)(128)(2,1)S(1)}, bf16[768]{0:T(1024)(128)(2,1)S(1)}, bf16[768]{0:T(1024)(128)(2,1)S(1)}, bf16[768]{0:T(1024)(128)(2,1)S(1)...) all-reduce(bf16[2304]{0:T(1024)(128)(2,1)S(1)} %dynamic-update-slic, ...), channel_id=1, replica_groups=mesh['replica'=2,'fsdp'=16] {'fsdp'}, use_global_device_ids=true, to_apply=%add | all-reduce | flops 9984 | bytes 39936
  101.6 4.3 all-to-all-start.2
  106.0 4.0 convolution_add_fusion
  110.4 1.9 copy-done.6
  117.2 5.0 fusion.35
  122.2 3.0 copy.65
  126.5 4.9 fusion.34
  131.5 2.8 copy.63
  136.1 4.3 fusion.4
  140.5 3.1 fusion.52
  144.9 6.1 fusion.68
  150.9 2.5 fusion.108
  154.4 12.6 %all-gather.9.cloned.1.call-done = bf16[768,3072]{1,0:T(8,128)(2,1)} async-done(((bf16[48,3072]{1,0:T(8,128)(2,1)}), bf16[768,3072]{1,0:T(8,128)(2,1)}) %all-gather.9.cloned.1.call-update) | async-done | bytes 4718608 | tf_op jit(solution)/shard_map/all_gather | solution.py:93
  167.0 20.1 %multiply_convert_fusion = (bf16[512,3072]{1,0:T(8,128)(2,1)}, f32[512,3072]{1,0:T(8,128)}, f32[512,3072]{1,0:T(8,128)}) fusion(f32[3072]{0:T(1024)} %convert_element_type.179, bf16[768,3072]{1,0:T(8,128)(2,1)} %all-gather.9.cloned.1.call-done, f32[512,768]{1,0:T(8,128)S(1)} %get-tuple-element.80, f32[768]{0:T(1024)} %convert_element_type.177, ...), kind=kOutput, calls=%fused_computation.41 | convolution fusion | flops 2521694208 | bytes 22042624 | tf_op jit(solution)/shard_map/dot_general | solution.py:17
  187.1 33.7 %all-gather.11.cloned.1.call-done = bf16[3072,768]{1,0:T(8,128)(2,1)} async-done(((bf16[192,768]{1,0:T(8,128)(2,1)}), bf16[3072,768]{1,0:T(8,128)(2,1)}) %all-gather.11.cloned.1.call-update) | async-done | bytes 4718608 | tf_op jit(solution)/shard_map/all_gather | solution.py:95
  220.8 6.1 fusion.109
  228.3 2.4 multiply_reduce_fusion.1
  231.4 3.0 fusion.105
  235.3 9.1 %convert_reduce_fusion = (f32[3072]{0:T(1024)}, bf16[512,3072]{1,0:T(8,128)(2,1)S(1)}) fusion(f32[512,3072]{1,0:T(8,128)} %get-tuple-element.61, f32[512,3072]{1,0:T(8,128)} %get-tuple-element.81, f32[3072]{0:T(1024)S(1)} %copy-done.48, bf16[512,768]{1,0:T(8,128)(2,1)S(1)} %get-tuple-element.49, bf16[3072,768]{1,0:T(8,128)(2,1)S(1)} %copy-done.62), kind=kOutput, calls=%fused_computation.39 | convolution fusion | flops 2442654720 | bytes 21258240 | tf_op jit(solution)/shard_map/dot_general | solution.py:27
  244.4 3.7 multiply_reduce_fusion.2
  250.4 2.1 fusion.113
  252.6 2.4 fusion.112
  257.2 3.1 fusion
  260.3 4.6 fusion.55
  265.2 3.8 fusion.36
  269.1 1.9 fusion.110
  272.9 1.8 fusion.38
  275.3 2.1 fusion.111
  280.0 5.1 bitcast_convert_fusion
  286.1 5.0 fusion.98
  291.8 7.2 fusion.99
  300.1 8.2 %fusion.114 = f32[3072,768]{1,0:T(8,128)} fusion(bf16[512,3072]{1,0:T(8,128)(2,1)} %get-tuple-element.60, bf16[512,768]{1,0:T(8,128)(2,1)S(1)} %copy-done.22), kind=kOutput, calls=%fused_computation.179 | convolution fusion | flops 2415919104 | bytes 13369344 | tf_op jit(solution)/shard_map/dot_general | solution.py:21
  308.3 3.8 all-to-all-start.1
  312.1 5.6 add_convert_fusion.1
  317.7 17.7 %all-to-all-done.1 = bf16[16,32,768]{2,1,0:T(8,128)(2,1)S(1)} async-done(((bf16[16,32,768]{2,1,0:T(8,128)(2,1)}), bf16[16,32,768]{2,1,0:T(8,128)(2,1)S(1)}, u32[]{:S(2)}, u32[]{:S(2)}) %all-to-all-start.1) | async-done | bytes 786464 | tf_op jit(solution)/shard_map/all_to_all | solution.py:281
  335.4 5.5 all-to-all-start.3
  341.0 85.3 %reduce-scatter.5.cloned.1.call-done = f32[48,2304]{1,0:T(8,128)} async-done(((f32[768,2304]{1,0:T(8,128)}), f32[48,2304]{1,0:T(8,128)}) %reduce-scatter.5.cloned.1.call-update) | async-done | bytes 442384 | tf_op jit(solution)/shard_map/reduce_scatter | solution.py:234
  426.3 115.0 %reduce-scatter.9.cloned.1.call-done = f32[48,3072]{1,0:T(8,128)} async-done(((f32[768,3072]{1,0:T(8,128)}), f32[48,3072]{1,0:T(8,128)}) %reduce-scatter.9.cloned.1.call-update) | async-done | bytes 589840 | tf_op jit(solution)/shard_map/reduce_scatter | solution.py:240
  541.3 115.0 %reduce-scatter.11.cloned.1.call-done = f32[192,768]{1,0:T(8,128)} async-done(((f32[3072,768]{1,0:T(8,128)}), f32[192,768]{1,0:T(8,128)}) %reduce-scatter.11.cloned.1.call-update) | async-done | bytes 589840 | tf_op jit(solution)/shard_map/reduce_scatter | solution.py:242
  660.4 1.5 convert_reduce_fusion.1
  662.0 60.3 %all-reduce.16 = (f32[2304]{0:T(1024)S(1)}, f32[768]{0:T(1024)S(1)}, f32[768]{0:T(1024)S(1)}, f32[768]{0:T(1024)S(1)}, f32[3072]{0:T(1024)S(1)}, /*index=5*/f32[...) all-reduce(f32[2304]{0:T(1024)S(1)} %convert_reduce_fusion.1, ...), channel_id=3, replica_groups=mesh['replica'=2,'fsdp'=16] {'fsdp'}, use_global_device_ids=true, to_apply=%region_19.21.clone | all-reduce | flops 9984 | bytes 79872
  722.9 5.5 all-reduce.17
  731.0 1.8 copy.111
  732.8 1.6 copy.112
  734.4 1.9 copy.113
  736.3 1.9 copy.114
  (276 shorter events, 43.2 us)
Async XLA Ops:
  7.2 5.4 copy-start.72
  7.2 98.8 %all-gather.5.cloned.1.call-start = ((), (), s32[]{:S(2)}) async-start(), calls=%async_computation.8 | async-start | bytes 3760128 | tf_op jit(solution)/shard_map/all_gather | solution.py:87
  7.9 143.0 %all-gather.7.cloned.1.call-start = ((), (), s32[]{:S(2)}) async-start(), calls=%async_computation.9 | async-start | bytes 1253376 | tf_op jit(solution)/shard_map/all_gather | solution.py:89
  8.7 158.3 %all-gather.9.cloned.1.call-start = ((), (), s32[]{:S(2)}) async-start(), calls=%async_computation.10 | async-start | bytes 5013504 | tf_op jit(solution)/shard_map/all_gather | solution.py:93
  10.7 11.3 %copy-start.61 = (u32[32]{0:T(128)S(1)}, u32[32]{0:T(128)}, u32[]{:S(2)}) copy-start(u32[32]{0:T(128)} %constant.105) | copy-start | bytes 388
  10.7 13.8 %copy-start.63 = (bf16[48]{0:T(256)(128)(2,1)S(1)}, bf16[48]{0:T(256)(128)(2,1)}, u32[]{:S(2)}) copy-start(bf16[48]{0:T(256)(128)(2,1)} %param.32) | copy-start | bytes 292
  10.7 14.1 %copy-start.64 = (bf16[48]{0:T(256)(128)(2,1)S(1)}, bf16[48]{0:T(256)(128)(2,1)}, u32[]{:S(2)}) copy-start(bf16[48]{0:T(256)(128)(2,1)} %param.30) | copy-start | bytes 292
  10.7 14.3 %copy-start.65 = (bf16[48]{0:T(256)(128)(2,1)S(1)}, bf16[48]{0:T(256)(128)(2,1)}, u32[]{:S(2)}) copy-start(bf16[48]{0:T(256)(128)(2,1)} %param.25) | copy-start | bytes 292
  10.8 14.5 %copy-start.66 = (bf16[48]{0:T(256)(128)(2,1)S(1)}, bf16[48]{0:T(256)(128)(2,1)}, u32[]{:S(2)}) copy-start(bf16[48]{0:T(256)(128)(2,1)} %param.26) | copy-start | bytes 292
  10.8 14.7 %copy-start.67 = (bf16[48]{0:T(256)(128)(2,1)S(1)}, bf16[48]{0:T(256)(128)(2,1)}, u32[]{:S(2)}) copy-start(bf16[48]{0:T(256)(128)(2,1)} %param.24) | copy-start | bytes 292
  10.8 14.9 %copy-start.68 = (bf16[48]{0:T(256)(128)(2,1)S(1)}, bf16[48]{0:T(256)(128)(2,1)}, u32[]{:S(2)}) copy-start(bf16[48]{0:T(256)(128)(2,1)} %param.31) | copy-start | bytes 292
  10.8 15.2 %copy-start.69 = (bf16[192]{0:T(256)(128)(2,1)S(1)}, bf16[192]{0:T(256)(128)(2,1)}, u32[]{:S(2)}) copy-start(bf16[192]{0:T(256)(128)(2,1)} %param.28) | copy-start | bytes 1156
  10.8 15.4 %copy-start.70 = (bf16[144]{0:T(256)(128)(2,1)S(1)}, bf16[144]{0:T(256)(128)(2,1)}, u32[]{:S(2)}) copy-start(bf16[144]{0:T(256)(128)(2,1)} %param.22) | copy-start | bytes 868
  10.8 89.9 %copy-start.71 = (s32[1,1,4]{2,1,0:T(1,128)S(1)}, s32[1,1,4]{2,1,0:T(1,128)}, u32[]{:S(2)}) copy-start(s32[1,1,4]{2,1,0:T(1,128)} %param.34) | copy-start | bytes 52
  14.0 87.6 %all-to-all-start = ((bf16[16,32,768]{2,1,0:T(8,128)(2,1)}), bf16[16,32,768]{2,1,0:T(8,128)(2,1)S(1)}, u32[]{:S(2)}, u32[]{:S(2)}) async-start(bf16[16,32,768]{2,1,0:T(8,128)(2,1)} %get-tuple-element.72), calls=%async_computation | async-start | bytes 1572864 | tf_op jit(solution)/shard_map/all_to_all | solution.py:81
  21.4 199.4 %all-gather.11.cloned.1.call-start = ((), (), s32[]{:S(2)}) async-start(), calls=%async_computation.11 | async-start | bytes 5013504 | tf_op jit(solution)/shard_map/all_gather | solution.py:95
  101.6 8.4 %copy-start.17 = (bf16[16,32,768]{2,1,0:T(8,128)(2,1)}, bf16[16,32,768]{2,1,0:T(8,128)(2,1)S(1)}, u32[]{:S(2)}) copy-start(bf16[16,32,768]{2,1,0:T(8,128)(2,1)S(1)} %all-to-all-done) | copy-start | bytes 2359300
  101.6 126.8 %all-to-all-start.2 = ((bf16[16,32,768]{2,1,0:T(8,128)(2,1)}), bf16[16,32,768]{2,1,0:T(8,128)(2,1)}, u32[]{:S(2)}, u32[]{:S(2)}) async-start(bf16[16,32,768]{2,1,0:T(8,128)(2,1)} %get-tuple-element.71), calls=%async_computation.2 | async-start | bytes 1572864 | tf_op jit(solution)/shard_map/all_to_all | solution.py:82
  105.9 235.1 %reduce-scatter.7.cloned.1.call-start = ((), (), s32[]{:S(2)}) async-start(), calls=%async_computation.13 | async-start | bytes 2506752 | tf_op jit(solution)/shard_map/reduce_scatter | solution.py:236
  126.5 5.0 copy-start.29
  135.2 5.3 copy-start.31
  144.8 6.1 copy-start.18
  153.4 67.3 %copy-start.39 = (f32[512]{0:T(512)}, f32[512]{0:T(512)S(1)}, u32[]{:S(2)}) copy-start(f32[512]{0:T(512)S(1)} %broadcast_multiply_fusion.3) | copy-start | bytes 6148
  154.3 32.7 %copy-start.50 = (f32[512]{0:T(512)}, f32[512]{0:T(512)S(1)}, u32[]{:S(2)}) copy-start(f32[512]{0:T(512)S(1)} %fusion.93) | copy-start | bytes 6148
  234.4 9.9 %slice-start.4 = ((s8[4718592]{0:T(1024)(128)(4,1)}), s8[4194304]{0:T(1024)(128)(4,1)S(1)}, s32[]{:S(2)}) async-start(s8[4718592]{0:T(1024)(128)(4,1)} %bitcast.213), calls=%async_computation.21 | async-start | bytes 8388608
  235.2 9.1 %copy-start.21 = (bf16[512,768]{1,0:T(8,128)(2,1)}, bf16[512,768]{1,0:T(8,128)(2,1)S(1)}, u32[]{:S(2)}) copy-start(bf16[512,768]{1,0:T(8,128)(2,1)S(1)} %get-tuple-element.49) | copy-start | bytes 2359300
  235.2 9.1 %copy-start.40 = (f32[512]{0:T(512)S(1)}, f32[512]{0:T(512)}, u32[]{:S(2)}) copy-start(f32[512]{0:T(512)} %copy-done.39) | copy-start | bytes 6148
  235.2 9.1 %copy-start.46 = (f32[768]{0:T(1024)S(1)}, f32[768]{0:T(1024)}, u32[]{:S(2)}) copy-start(f32[768]{0:T(1024)} %convert_element_type.176) | copy-start | bytes 9220
  235.2 9.1 %copy-start.51 = (f32[512]{0:T(512)S(1)}, f32[512]{0:T(512)}, u32[]{:S(2)}) copy-start(f32[512]{0:T(512)} %copy-done.50) | copy-start | bytes 6148
  235.3 9.1 %slice-start.5 = ((s8[4718592]{0:T(1024)(128)(4,1)}), s8[524288]{0:T(1024)(128)(4,1)S(1)}, s32[]{:S(2)}) async-start(s8[4718592]{0:T(1024)(128)(4,1)} %bitcast.213), calls=%async_computation.22 | async-start | bytes 1048576
  255.5 4.8 copy-start.26
  264.9 161.3 %reduce-scatter.5.cloned.1.call-start = ((), (), s32[]{:S(2)}) async-start(), calls=%async_computation.12 | async-start | bytes 7520256 | tf_op jit(solution)/shard_map/reduce_scatter | solution.py:234
  272.9 12.3 %copy-start.11 = (bf16[512,12,64]{0,2,1:T(8,128)(2,1)}, bf16[512,12,64]{0,2,1:T(8,128)(2,1)S(1)}, u32[]{:S(2)}) copy-start(bf16[512,12,64]{0,2,1:T(8,128)(2,1)S(1)} %fusion.61) | copy-start | bytes 2359300
  280.0 5.2 copy-start.13
  280.0 6.0 copy-start.19
  291.1 250.2 %reduce-scatter.9.cloned.1.call-start = ((), (), s32[]{:S(2)}) async-start(), calls=%async_computation.14 | async-start | bytes 10027008 | tf_op jit(solution)/shard_map/reduce_scatter | solution.py:240
  299.0 357.3 %reduce-scatter.11.cloned.1.call-start = ((), (), s32[]{:S(2)}) async-start(), calls=%async_computation.15 | async-start | bytes 10027008 | tf_op jit(solution)/shard_map/reduce_scatter | solution.py:242
  308.3 27.1 %all-to-all-start.1 = ((bf16[16,32,768]{2,1,0:T(8,128)(2,1)}), bf16[16,32,768]{2,1,0:T(8,128)(2,1)S(1)}, u32[]{:S(2)}, u32[]{:S(2)}) async-start(bf16[16,32,768]{2,1,0:T(8,128)(2,1)} %bitcast.192), calls=%async_computation.1 | async-start | bytes 1572864 | tf_op jit(solution)/shard_map/all_to_all | solution.py:281
  317.7 340.6 %copy-start.73 = (s32[1,16]{1,0:T(1,128)S(1)}, s32[1,16]{1,0:T(1,128)}, u32[]{:S(2)}) copy-start(s32[1,16]{1,0:T(1,128)} %param.35) | copy-start | bytes 196
  317.7 342.7 %copy-start.14 = (bf16[512,12,64]{0,2,1:T(8,128)(2,1)S(1)}, bf16[512,12,64]{0,2,1:T(8,128)(2,1)}, u32[]{:S(2)}) copy-start(bf16[512,12,64]{0,2,1:T(8,128)(2,1)} %copy-done.13) | copy-start | bytes 2359300
  335.4 326.5 %copy-start.44 = (f32[768]{0:T(1024)S(1)}, f32[768]{0:T(1024)}, u32[]{:S(2)}) copy-start(f32[768]{0:T(1024)} %get-tuple-element.17) | copy-start | bytes 9220
  335.4 326.6 %copy-start.45 = (f32[768]{0:T(1024)S(1)}, f32[768]{0:T(1024)}, u32[]{:S(2)}) copy-start(f32[768]{0:T(1024)} %get-tuple-element.48) | copy-start | bytes 9220
  335.4 326.6 %copy-start.49 = (f32[3072]{0:T(1024)S(1)}, f32[3072]{0:T(1024)}, u32[]{:S(2)}) copy-start(f32[3072]{0:T(1024)} %get-tuple-element.50) | copy-start | bytes 36868
  335.4 326.6 %copy-start.58 = (f32[768]{0:T(1024)S(1)}, f32[768]{0:T(1024)}, u32[]{:S(2)}) copy-start(f32[768]{0:T(1024)} %get-tuple-element.15) | copy-start | bytes 9220
  335.4 326.6 %copy-start.59 = (f32[768]{0:T(1024)S(1)}, f32[768]{0:T(1024)}, u32[]{:S(2)}) copy-start(f32[768]{0:T(1024)} %get-tuple-element.19) | copy-start | bytes 9220
  335.4 393.6 %all-to-all-start.3 = ((bf16[16,32,768]{2,1,0:T(8,128)(2,1)}), bf16[16,32,768]{2,1,0:T(8,128)(2,1)S(1)}, u32[]{:S(2)}, u32[]{:S(2)}) async-start(bf16[16,32,768]{2,1,0:T(8,128)(2,1)} %bitcast.200), calls=%async_computation.3 | async-start | bytes 1572864 | tf_op jit(solution)/shard_map/all_to_all | solution.py:282
  340.9 390.1 %all-reduce.22.cloned.1.call-start = ((), (), s32[]{:S(2)}) async-start(), calls=%async_computation.16 | async-start | bytes 3538944 | tf_op jit(solution)/shard_map/psum | solution.py:261
  729.0 9.2 %copy-start.1 = (bf16[512,768]{1,0:T(8,128)(2,1)S(1)}, bf16[512,768]{1,0:T(8,128)(2,1)}, u32[]{:S(2)}) copy-start(bf16[512,768]{1,0:T(8,128)(2,1)} %param.20) | copy-start | bytes 2359300
  (49 other events, 119.4 us)
Sparse Core Ops, SparseCore 0:
  10.3 59.1 all-gather.4
  71.8 37.0 all-gather.6
  111.2 55.7 all-gather.8
  169.1 51.6 all-gather.10
  265.1 67.9 reduce-scatter.6
  337.0 89.2 reduce-scatter.4
  430.4 110.8 reduce-scatter.8
  545.4 110.8 reduce-scatter.10
  658.8 55.4 all-reduce.21
where the time goes:
time: 753 us; the launch traced here: 745 us
  waiting for transfers between devices  382 us (51%)
  blocking collectives  137 us (18%)
  matrix products  124 us (16%)
  local copies, waits for them, and re-layouts  38.5 us (5%)
  other arithmetic  22.6 us (3%)
  starting transfers between devices  21.8 us (3%)
  between operations  19.2 us (3%)
    unnamed x2, blocking collectives  132 us
    reduce_scatter x1, waiting for transfers between devices, body(): lax.psum_scatter(grad_weight_inner, 'fsdp', scatter_dimension=0, tiled=True)  115 us
    reduce_scatter x1, waiting for transfers between devices, body(): lax.psum_scatter(grad_weight_outer, 'fsdp', scatter_dimension=0, tiled=True)  115 us
    reduce_scatter x1, waiting for transfers between devices, body(): lax.psum_scatter(grad_weight_qkv, 'fsdp', scatter_dimension=0, tiled=True)  85.3 us
    all_gather x1, waiting for transfers between devices, body(): lax.all_gather(outer_weight, 'fsdp', axis=0, tiled=True)  33.7 us
    dot_general x4, matrix products, matrix_product(): return jnp.dot(left, right, preferred_element_type=jnp.float32)  32.7 us
    unnamed x197, local copies, waits for them, and re-layouts  24.3 us
    dot_general x4, matrix products, rows_product(): lax.dot_general(left, right, (((0,), (0,)), ((), ())), preferred_element_...  22.6 us
  transfers between devices with their start and end apart: 13, of which 6 were waited for; matrix products, arithmetic and copies ran while one was open for 17% of the time, Pallas kernels for 0%

commit v1 on v0

--- a/solution.py
+++ b/solution.py
@@ -5,6 +5,27 @@
 from jax.sharding import PartitionSpec as P
 
 EPSILON = 1e-06
+
+
+def ring_gather(shard, axis, dim):
+    size, here, extent = (lax.axis_size(axis), lax.axis_index(axis), shard.shape[dim])
+    forward = [(i, (i + 1) % size) for i in range(size)]
+    backward = [(i, (i - 1) % size) for i in range(size)]
+    out = jnp.zeros((*shard.shape[:dim], size * extent, *shard.shape[dim + 1 :]), shard.dtype)
+    out = lax.dynamic_update_slice_in_dim(out, shard, here * extent, axis=dim)
+    from_left = from_right = shard
+    middle = size // 2
+    for lap in range(1, middle + 1):
+        from_left = lax.ppermute(from_left, axis, forward)
+        out = lax.dynamic_update_slice_in_dim(
+            out, from_left, (here - lap) % size * extent, axis=dim
+        )
+        if lap < size - middle:
+            from_right = lax.ppermute(from_right, axis, backward)
+            out = lax.dynamic_update_slice_in_dim(
+                out, from_right, (here + lap) % size * extent, axis=dim
+            )
+    return out
 
 
 def layer_norm(summed, gain_vec, shift_vec):
@@ -92,7 +113,7 @@
         lax.all_gather(attn_shift, "fsdp", axis=0, tiled=True),
         lax.all_gather(inner_weight, "fsdp", axis=0, tiled=True),
         lax.all_gather(inner_bias, "fsdp", axis=0, tiled=True),
-        lax.all_gather(outer_weight, "fsdp", axis=0, tiled=True),
+        ring_gather(outer_weight, "fsdp", 0),
         lax.all_gather(outer_bias, "fsdp", axis=0, tiled=True),
         lax.all_gather(ffn_gain, "fsdp", axis=0, tiled=True),
         lax.all_gather(ffn_shift, "fsdp", axis=0, tiled=True),

time: 753 us -> 785 us (1.042)
  waiting for transfers between devices: 382 us -> 351 us
  starting transfers between devices: 21.8 us -> 44.6 us
  blocking collectives: 137 us -> 155 us
  local copies, waits for them, and re-layouts: 38.5 us -> 52.2 us
  matrix products: 124 us -> 132 us
    ppermute x0 -> x15, waiting for transfers between devices: none -> 40.5 us  [the longest x7 35.1 us: ring_gather(): from_right = lax.ppermute(from_right, axis, backward)]
    all_gather x1, waiting for transfers between devices: 33.7 us -> 0.01 us  [body(): lax.all_gather(outer_weight, 'fsdp', axis=0, tiled=True)]
    ppermute x0 -> x15, starting transfers between devices: none -> 29 us  [the longest x7 27.8 us: ring_gather(): from_right = lax.ppermute(from_right, axis, backward)]
    all_to_all x0 -> x1, blocking collectives: none -> 26.9 us  [body(): lax.all_to_all(grad_rows, 'fsdp', split_axis=0, concat_axis=0, tiled=True)]
    all_to_all x1, waiting for transfers between devices: 17.7 us -> 0.01 us  [body(): lax.all_to_all(out_rows, 'fsdp', split_axis=0, concat_axis=0, tiled=True)]
    all_gather x1, waiting for transfers between devices: 12.6 us -> 0.01 us  [body(): lax.all_gather(inner_weight, 'fsdp', axis=0, tiled=True)]
    dynamic_update_slice x0 -> x16, local copies, waits for them, and re-layouts: none -> 11.8 us  [the longest x8 5.9 us: ring_gather(): lax.dynamic_update_slice_in_dim(out, from_left, (here - lap) % size * ext...]
    unnamed x2, blocking collectives: 132 us -> 123 us
  transfers between devices with their start and end apart: 13 -> 27, of which waited for: 6 -> 11; matrix products, arithmetic and copies ran while one was open for 17% -> 21% of each run, Pallas kernels for 0% -> 0%
where the time goes in v1:
time: 785 us; the launch traced here: 776 us
  waiting for transfers between devices  351 us (45%)
  blocking collectives  155 us (20%)
  matrix products  132 us (17%)
  local copies, waits for them, and re-layouts  52.2 us (7%)
  starting transfers between devices  44.6 us (6%)
  other arithmetic  22.2 us (3%)
  between operations  19 us (2%)
    unnamed x2, blocking collectives  123 us
    reduce_scatter x1, waiting for transfers between devices, body(): lax.psum_scatter(grad_weight_outer, 'fsdp', scatter_dimension=0, tiled=True)  115 us
    reduce_scatter x1, waiting for transfers between devices, body(): lax.psum_scatter(grad_weight_inner, 'fsdp', scatter_dimension=0, tiled=True)  115 us
    reduce_scatter x1, waiting for transfers between devices, body(): lax.psum_scatter(grad_weight_qkv, 'fsdp', scatter_dimension=0, tiled=True)  77.4 us
    ppermute x7, waiting for transfers between devices, ring_gather(): from_right = lax.ppermute(from_right, axis, backward)  35.1 us
    dot_general x4, matrix products, matrix_product(): return jnp.dot(left, right, preferred_element_type=jnp.float32)  32.4 us
    ppermute x7, starting transfers between devices, ring_gather(): from_right = lax.ppermute(from_right, axis, backward)  27.8 us
    all_to_all x1, blocking collectives, body(): lax.all_to_all(grad_rows, 'fsdp', split_axis=0, concat_axis=0, tiled=True)  26.9 us
  transfers between devices with their start and end apart: 27, of which 11 were waited for; matrix products, arithmetic and copies ran while one was open for 21% of the time, Pallas kernels for 0%

profile of v1, /device:TPU:0, one launch (start us, length us, event | category | flops | bytes accessed | tf_op | source)
XLA Modules:
  0.0 776.1 jit_solution(18402903235834963941)
XLA Ops:
  10.0 5.0 collective-permute-start.1
  21.1 6.9 all-to-all-start
  28.8 4.3 collective-permute-start.3
  33.9 16.8 %collective-permute-done.3 = bf16[192,768]{1,0:T(8,128)(2,1)S(1)} collective-permute-done((bf16[192,768]{1,0:T(8,128)(2,1)S(1)}, bf16[192,768]{1,0:T(8,128)(2,1)S(1)}, u32[]{:S(2)}, u32[]{:S(2)}) %collective-permute-start.3) | collective-permute-done | bytes 294944 | tf_op jit(solution)/shard_map/ppermute | solution.py:24
  50.7 4.6 collective-permute-start.5
  55.3 2.4 broadcast_in_dim.19
  63.0 62.3 %all-reduce.19 = (bf16[2304]{0:T(1024)(128)(2,1)S(1)}, bf16[768]{0:T(1024)(128)(2,1)S(1)}, bf16[768]{0:T(1024)(128)(2,1)S(1)}, bf16[768]{0:T(1024)(128)(2,1)S(1)...) all-reduce(bf16[2304]{0:T(1024)(128)(2,1)S(1)} %dynamic-update-slic, ...), channel_id=1, replica_groups=mesh['replica'=2,'fsdp'=16] {'fsdp'}, use_global_device_ids=true, to_apply=%add | all-reduce | flops 9984 | bytes 39936
  131.8 6.7 collective-permute-done.7
  138.5 4.6 collective-permute-start.9
  145.3 4.9 collective-permute-done.9
  150.1 4.6 collective-permute-start.11
  157.8 3.6 collective-permute-done.11
  161.4 4.6 collective-permute-start.13
  168.2 3.2 collective-permute-done.13
  172.1 3.7 collective-permute-done.14
  176.5 4.3 all-to-all-start.2
  180.9 4.0 convolution_add_fusion
  188.6 4.9 fusion.34
  195.0 3.2 copy.63
  203.0 4.9 fusion.35
  207.9 2.8 copy.65
  212.2 5.3 fusion.52
  217.5 4.3 fusion.4
  222.4 6.0 fusion.68
  228.5 2.5 fusion.108
  231.9 19.7 %multiply_convert_fusion = (bf16[512,3072]{1,0:T(8,128)(2,1)S(1)}, f32[512,3072]{1,0:T(8,128)}, f32[512,3072]{1,0:T(8,128)}) fusion(f32[3072]{0:T(1024)} %convert_element_type.179, bf16[768,3072]{1,0:T(8,128)(2,1)} %all-gather.9.cloned.1.call-done, f32[512,768]{1,0:T(8,128)S(1)} %get-tuple-element.80, f32[768]{0:T(1024)} %convert_element_type.177, ...), kind=kOutput, calls=%fused_computation.41 | convolution fusion | flops 2521694208 | bytes 22042624 | tf_op jit(solution)/shard_map/dot_general | solution.py:38
  251.7 6.2 fusion.109
  259.3 2.4 multiply_reduce_fusion.1
  262.4 2.8 fusion.105
  267.2 9.3 %convert_reduce_fusion = (f32[3072]{0:T(1024)}, bf16[512,3072]{1,0:T(8,128)(2,1)S(1)}) fusion(f32[512,3072]{1,0:T(8,128)} %get-tuple-element.61, f32[512,3072]{1,0:T(8,128)} %get-tuple-element.81, f32[3072]{0:T(1024)} %convert_element_type.179, bf16[512,768]{1,0:T(8,128)(2,1)S(1)} %get-tuple-element.49, bf16[3072,768]{1,0:T(8,128)(2,1)} %all-gather.11.cloned.1.call-done), kind=kOutput, calls=%fused_computation.39 | convolution fusion | flops 2442654720 | bytes 21258240 | tf_op jit(solution)/shard_map/dot_general | solution.py:48
  276.6 7.2 multiply_reduce_fusion.2
  288.3 2.5 fusion.112
  291.3 4.5 fusion.38
  296.5 6.3 fusion.111
  302.9 3.3 fusion.55
  309.3 2.5 fusion
  315.6 5.3 bitcast_convert_fusion
  321.8 5.0 fusion.98
  326.9 8.4 %fusion.114 = f32[3072,768]{1,0:T(8,128)} fusion(bf16[512,3072]{1,0:T(8,128)(2,1)} %copy-done.76, bf16[512,768]{1,0:T(8,128)(2,1)} %copy-done.26), kind=kOutput, calls=%fused_computation.195 | convolution fusion | flops 2415919104 | bytes 13369344 | tf_op jit(solution)/shard_map/dot_general | solution.py:42
  336.0 7.2 fusion.99
  344.6 4.3 add_convert_fusion.1
  348.9 26.9 %all_to_all.20 = bf16[16,32,768]{2,1,0:T(8,128)(2,1)S(1)} all-to-all(bf16[16,32,768]{2,1,0:T(8,128)(2,1)S(1)} %bitcast.197), channel_id=1, replica_groups=mesh['replica'=2,'fsdp'=16] {'fsdp'}, dimensions={0} | all-to-all | bytes 1572864 | tf_op jit(solution)/shard_map/all_to_all | solution.py:303
  375.8 4.1 all-to-all-start.1
  380.0 77.4 %reduce-scatter.5.cloned.1.call-done = f32[48,2304]{1,0:T(8,128)} async-done(((f32[768,2304]{1,0:T(8,128)}), f32[48,2304]{1,0:T(8,128)}) %reduce-scatter.5.cloned.1.call-update) | async-done | bytes 442384 | tf_op jit(solution)/shard_map/reduce_scatter | solution.py:255
  457.4 115.0 %reduce-scatter.11.cloned.1.call-done = f32[192,768]{1,0:T(8,128)} async-done(((f32[3072,768]{1,0:T(8,128)}), f32[192,768]{1,0:T(8,128)}) %reduce-scatter.11.cloned.1.call-update) | async-done | bytes 589840 | tf_op jit(solution)/shard_map/reduce_scatter | solution.py:263
  572.4 115.0 %reduce-scatter.9.cloned.1.call-done = f32[48,3072]{1,0:T(8,128)} async-done(((f32[768,3072]{1,0:T(8,128)}), f32[48,3072]{1,0:T(8,128)}) %reduce-scatter.9.cloned.1.call-update) | async-done | bytes 589840 | tf_op jit(solution)/shard_map/reduce_scatter | solution.py:261
  693.1 60.3 %all-reduce.16 = (f32[2304]{0:T(1024)S(1)}, f32[768]{0:T(1024)S(1)}, f32[768]{0:T(1024)S(1)}, f32[768]{0:T(1024)S(1)}, f32[3072]{0:T(1024)S(1)}, /*index=5*/f32[...) all-reduce(f32[2304]{0:T(1024)S(1)} %convert_reduce_fusion.1, ...), channel_id=3, replica_groups=mesh['replica'=2,'fsdp'=16] {'fsdp'}, use_global_device_ids=true, to_apply=%region_19.21.clone | all-reduce | flops 9984 | bytes 79872
  754.0 5.7 all-reduce.17
  (316 shorter events, 75.3 us)
Async XLA Ops:
  7.2 21.4 %copy-start.66 = (s32[1,1,4]{2,1,0:T(1,128)S(1)}, s32[1,1,4]{2,1,0:T(1,128)}, u32[]{:S(2)}) copy-start(s32[1,1,4]{2,1,0:T(1,128)} %param.34) | copy-start | bytes 52
  7.2 173.7 %all-gather.5.cloned.1.call-start = ((), (), s32[]{:S(2)}) async-start(), calls=%async_computation.8 | async-start | bytes 3760128 | tf_op jit(solution)/shard_map/all_gather | solution.py:108
  7.9 220.5 %all-gather.7.cloned.1.call-start = ((), (), s32[]{:S(2)}) async-start(), calls=%async_computation.9 | async-start | bytes 1253376 | tf_op jit(solution)/shard_map/all_gather | solution.py:110
  8.7 223.2 %all-gather.9.cloned.1.call-start = ((), (), s32[]{:S(2)}) async-start(), calls=%async_computation.10 | async-start | bytes 5013504 | tf_op jit(solution)/shard_map/all_gather | solution.py:114
  9.4 10.3 %collective-permute-start = (bf16[192,768]{1,0:T(8,128)(2,1)}, bf16[192,768]{1,0:T(8,128)(2,1)S(1)}, u32[]{:S(2)}, u32[]{:S(2)}) collective-permute-start(bf16[192,768]{1,0:T(8,128)(2,1)} %param.29), channel_id=1, source_target_pairs={{0,1},{1,2},{2,3},{3,4},{4,5},{5,6},{6,7},{7,8},{8,9},{9,10},{10,1... | collective-permute-start | bytes 884744 | tf_op jit(solution)/shard_map/ppermute | solution.py:19
  10.0 18.8 %collective-permute-start.1 = (bf16[192,768]{1,0:T(8,128)(2,1)}, bf16[192,768]{1,0:T(8,128)(2,1)S(1)}, u32[]{:S(2)}, u32[]{:S(2)}) collective-permute-start(bf16[192,768]{1,0:T(8,128)(2,1)} %param.29), channel_id=1, source_target_pairs={{0,15},{1,0},{2,1},{3,2},{4,3},{5,4},{6,5},{7,6},{8,7},{9,8},{10,9... | collective-permute-start | bytes 884744 | tf_op jit(solution)/shard_map/ppermute | solution.py:24
  18.7 39.1 %copy-start.20 = (bf16[192,768]{1,0:T(8,128)(2,1)S(1)}, bf16[192,768]{1,0:T(8,128)(2,1)}, u32[]{:S(2)}) copy-start(bf16[192,768]{1,0:T(8,128)(2,1)} %param.29) | copy-start | bytes 884740
  18.7 39.8 %copy-start.65 = (u32[32]{0:T(128)S(1)}, u32[32]{0:T(128)}, u32[]{:S(2)}) copy-start(u32[32]{0:T(128)} %constant.212) | copy-start | bytes 388
  18.7 42.3 %copy-start.67 = (bf16[48]{0:T(256)(128)(2,1)S(1)}, bf16[48]{0:T(256)(128)(2,1)}, u32[]{:S(2)}) copy-start(bf16[48]{0:T(256)(128)(2,1)} %param.24) | copy-start | bytes 292
  18.7 42.6 %copy-start.68 = (bf16[48]{0:T(256)(128)(2,1)S(1)}, bf16[48]{0:T(256)(128)(2,1)}, u32[]{:S(2)}) copy-start(bf16[48]{0:T(256)(128)(2,1)} %param.25) | copy-start | bytes 292
  18.7 42.8 %copy-start.69 = (bf16[48]{0:T(256)(128)(2,1)S(1)}, bf16[48]{0:T(256)(128)(2,1)}, u32[]{:S(2)}) copy-start(bf16[48]{0:T(256)(128)(2,1)} %param.26) | copy-start | bytes 292
  18.7 43.0 %copy-start.70 = (bf16[48]{0:T(256)(128)(2,1)S(1)}, bf16[48]{0:T(256)(128)(2,1)}, u32[]{:S(2)}) copy-start(bf16[48]{0:T(256)(128)(2,1)} %param.30) | copy-start | bytes 292
  18.8 43.2 %copy-start.71 = (bf16[48]{0:T(256)(128)(2,1)S(1)}, bf16[48]{0:T(256)(128)(2,1)}, u32[]{:S(2)}) copy-start(bf16[48]{0:T(256)(128)(2,1)} %param.31) | copy-start | bytes 292
  18.8 43.5 %copy-start.72 = (bf16[48]{0:T(256)(128)(2,1)S(1)}, bf16[48]{0:T(256)(128)(2,1)}, u32[]{:S(2)}) copy-start(bf16[48]{0:T(256)(128)(2,1)} %param.32) | copy-start | bytes 292
  18.8 43.7 %copy-start.73 = (bf16[144]{0:T(256)(128)(2,1)S(1)}, bf16[144]{0:T(256)(128)(2,1)}, u32[]{:S(2)}) copy-start(bf16[144]{0:T(256)(128)(2,1)} %param.22) | copy-start | bytes 868
  18.8 43.9 %copy-start.74 = (bf16[192]{0:T(256)(128)(2,1)S(1)}, bf16[192]{0:T(256)(128)(2,1)}, u32[]{:S(2)}) copy-start(bf16[192]{0:T(256)(128)(2,1)} %param.28) | copy-start | bytes 1156
  19.7 13.6 %collective-permute-start.2 = (bf16[192,768]{1,0:T(8,128)(2,1)S(1)}, bf16[192,768]{1,0:T(8,128)(2,1)S(1)}, u32[]{:S(2)}, u32[]{:S(2)}) collective-permute-start(bf16[192,768]{1,0:T(8,128)(2,1)S(1)} %collective-permute-done), channel_id=1, source_target_pairs={{0,1},{1,2},{2,3},{3,4},{4,5},{5,6},{6,7},{7,8},{8,9},{9,10},{10,1... | collective-permute-start | bytes 884744 | tf_op jit(solution)/shard_map/ppermute | solution.py:19
  21.1 155.4 %all-to-all-start = ((bf16[16,32,768]{2,1,0:T(8,128)(2,1)}), bf16[16,32,768]{2,1,0:T(8,128)(2,1)S(1)}, u32[]{:S(2)}, u32[]{:S(2)}) async-start(bf16[16,32,768]{2,1,0:T(8,128)(2,1)} %get-tuple-element.72), calls=%async_computation | async-start | bytes 1572864 | tf_op jit(solution)/shard_map/all_to_all | solution.py:102
  28.0 239.2 %all-gather.11.cloned.1.call-start = ((), (), s32[]{:S(2)}) async-start(), calls=%async_computation.11 | async-start | bytes 5013504 | tf_op jit(solution)/shard_map/all_gather | solution.py:194
  28.8 21.9 %collective-permute-start.3 = (bf16[192,768]{1,0:T(8,128)(2,1)S(1)}, bf16[192,768]{1,0:T(8,128)(2,1)S(1)}, u32[]{:S(2)}, u32[]{:S(2)}) collective-permute-start(bf16[192,768]{1,0:T(8,128)(2,1)S(1)} %collective-permute-done.1), channel_id=1, source_target_pairs={{0,15},{1,0},{2,1},{3,2},{4,3},{5,4},{6,5},{7,6},{8,7},{9,8},{10,9... | collective-permute-start | bytes 884744 | tf_op jit(solution)/shard_map/ppermute | solution.py:24
  33.3 22.1 %collective-permute-start.4 = (bf16[192,768]{1,0:T(8,128)(2,1)S(1)}, bf16[192,768]{1,0:T(8,128)(2,1)S(1)}, u32[]{:S(2)}, u32[]{:S(2)}) collective-permute-start(bf16[192,768]{1,0:T(8,128)(2,1)S(1)} %collective-permute-done.2), channel_id=1, source_target_pairs={{0,1},{1,2},{2,3},{3,4},{4,5},{5,6},{6,7},{7,8},{8,9},{9,10},{10,1... | collective-permute-start | bytes 884744 | tf_op jit(solution)/shard_map/ppermute | solution.py:19
  50.7 78.4 %collective-permute-start.5 = (bf16[192,768]{1,0:T(8,128)(2,1)S(1)}, bf16[192,768]{1,0:T(8,128)(2,1)S(1)}, u32[]{:S(2)}, u32[]{:S(2)}) collective-permute-start(bf16[192,768]{1,0:T(8,128)(2,1)S(1)} %collective-permute-done.3), channel_id=1, source_target_pairs={{0,15},{1,0},{2,1},{3,2},{4,3},{5,4},{6,5},{7,6},{8,7},{9,8},{10,9... | collective-permute-start | bytes 884744 | tf_op jit(solution)/shard_map/ppermute | solution.py:24
  55.3 74.5 %collective-permute-start.6 = (bf16[192,768]{1,0:T(8,128)(2,1)S(1)}, bf16[192,768]{1,0:T(8,128)(2,1)S(1)}, u32[]{:S(2)}, u32[]{:S(2)}) collective-permute-start(bf16[192,768]{1,0:T(8,128)(2,1)S(1)} %collective-permute-done.4), channel_id=1, source_target_pairs={{0,1},{1,2},{2,3},{3,4},{4,5},{5,6},{6,7},{7,8},{8,9},{9,10},{10,1... | collective-permute-start | bytes 884744 | tf_op jit(solution)/shard_map/ppermute | solution.py:19
  129.1 9.4 %collective-permute-start.7 = (bf16[192,768]{1,0:T(8,128)(2,1)S(1)}, bf16[192,768]{1,0:T(8,128)(2,1)S(1)}, u32[]{:S(2)}, u32[]{:S(2)}) collective-permute-start(bf16[192,768]{1,0:T(8,128)(2,1)S(1)} %collective-permute-done.5), channel_id=1, source_target_pairs={{0,15},{1,0},{2,1},{3,2},{4,3},{5,4},{6,5},{7,6},{8,7},{9,8},{10,9... | collective-permute-start | bytes 884744 | tf_op jit(solution)/shard_map/ppermute | solution.py:24
  129.8 14.0 %collective-permute-start.8 = (bf16[192,768]{1,0:T(8,128)(2,1)S(1)}, bf16[192,768]{1,0:T(8,128)(2,1)S(1)}, u32[]{:S(2)}, u32[]{:S(2)}) collective-permute-start(bf16[192,768]{1,0:T(8,128)(2,1)S(1)} %collective-permute-done.6), channel_id=1, source_target_pairs={{0,1},{1,2},{2,3},{3,4},{4,5},{5,6},{6,7},{7,8},{8,9},{9,10},{10,1... | collective-permute-start | bytes 884744 | tf_op jit(solution)/shard_map/ppermute | solution.py:19
  138.5 11.7 %collective-permute-start.9 = (bf16[192,768]{1,0:T(8,128)(2,1)S(1)}, bf16[192,768]{1,0:T(8,128)(2,1)S(1)}, u32[]{:S(2)}, u32[]{:S(2)}) collective-permute-start(bf16[192,768]{1,0:T(8,128)(2,1)S(1)} %collective-permute-done.7), channel_id=1, source_target_pairs={{0,15},{1,0},{2,1},{3,2},{4,3},{5,4},{6,5},{7,6},{8,7},{9,8},{10,9... | collective-permute-start | bytes 884744 | tf_op jit(solution)/shard_map/ppermute | solution.py:24
  143.8 12.5 %collective-permute-start.10 = (bf16[192,768]{1,0:T(8,128)(2,1)S(1)}, bf16[192,768]{1,0:T(8,128)(2,1)S(1)}, u32[]{:S(2)}, u32[]{:S(2)}) collective-permute-start(bf16[192,768]{1,0:T(8,128)(2,1)S(1)} %collective-permute-done.8), channel_id=1, source_target_pairs={{0,1},{1,2},{2,3},{3,4},{4,5},{5,6},{6,7},{7,8},{8,9},{9,10},{10,1... | collective-permute-start | bytes 884744 | tf_op jit(solution)/shard_map/ppermute | solution.py:19
  150.1 11.3 %collective-permute-start.11 = (bf16[192,768]{1,0:T(8,128)(2,1)S(1)}, bf16[192,768]{1,0:T(8,128)(2,1)S(1)}, u32[]{:S(2)}, u32[]{:S(2)}) collective-permute-start(bf16[192,768]{1,0:T(8,128)(2,1)S(1)} %collective-permute-done.9), channel_id=1, source_target_pairs={{0,15},{1,0},{2,1},{3,2},{4,3},{5,4},{6,5},{7,6},{8,7},{9,8},{10,9... | collective-permute-start | bytes 884744 | tf_op jit(solution)/shard_map/ppermute | solution.py:24
  156.3 10.4 %collective-permute-start.12 = (bf16[192,768]{1,0:T(8,128)(2,1)S(1)}, bf16[192,768]{1,0:T(8,128)(2,1)S(1)}, u32[]{:S(2)}, u32[]{:S(2)}) collective-permute-start(bf16[192,768]{1,0:T(8,128)(2,1)S(1)} %collective-permute-done.10), channel_id=1, source_target_pairs={{0,1},{1,2},{2,3},{3,4},{4,5},{5,6},{6,7},{7,8},{8,9},{9,10},{10,1... | collective-permute-start | bytes 884744 | tf_op jit(solution)/shard_map/ppermute | solution.py:19
  161.4 10.0 %collective-permute-start.13 = (bf16[192,768]{1,0:T(8,128)(2,1)S(1)}, bf16[192,768]{1,0:T(8,128)(2,1)S(1)}, u32[]{:S(2)}, u32[]{:S(2)}) collective-permute-start(bf16[192,768]{1,0:T(8,128)(2,1)S(1)} %collective-permute-done.11), channel_id=1, source_target_pairs={{0,15},{1,0},{2,1},{3,2},{4,3},{5,4},{6,5},{7,6},{8,7},{9,8},{10,9... | collective-permute-start | bytes 884744 | tf_op jit(solution)/shard_map/ppermute | solution.py:24
  166.7 9.0 %collective-permute-start.14 = (bf16[192,768]{1,0:T(8,128)(2,1)S(1)}, bf16[192,768]{1,0:T(8,128)(2,1)S(1)}, u32[]{:S(2)}, u32[]{:S(2)}) collective-permute-start(bf16[192,768]{1,0:T(8,128)(2,1)S(1)} %collective-permute-done.12), channel_id=1, source_target_pairs={{0,1},{1,2},{2,3},{3,4},{4,5},{5,6},{6,7},{7,8},{8,9},{9,10},{10,1... | collective-permute-start | bytes 884744 | tf_op jit(solution)/shard_map/ppermute | solution.py:19
  176.5 82.8 %all-to-all-start.2 = ((bf16[16,32,768]{2,1,0:T(8,128)(2,1)}), bf16[16,32,768]{2,1,0:T(8,128)(2,1)}, u32[]{:S(2)}, u32[]{:S(2)}) async-start(bf16[16,32,768]{2,1,0:T(8,128)(2,1)} %get-tuple-element.71), calls=%async_computation.2 | async-start | bytes 1572864 | tf_op jit(solution)/shard_map/all_to_all | solution.py:103
  180.8 199.1 %reduce-scatter.7.cloned.1.call-start = ((), (), s32[]{:S(2)}) async-start(), calls=%async_computation.13 | async-start | bytes 2506752 | tf_op jit(solution)/shard_map/reduce_scatter | solution.py:257
  228.5 23.2 %copy-start.28 = (bf16[512,12,64]{0,2,1:T(8,128)(2,1)}, bf16[512,12,64]{0,2,1:T(8,128)(2,1)S(1)}, u32[]{:S(2)}) copy-start(bf16[512,12,64]{0,2,1:T(8,128)(2,1)S(1)} %get-tuple-element.77) | copy-start | bytes 2359300
  231.0 20.6 %copy-start.40 = (f32[512]{0:T(512)}, f32[512]{0:T(512)S(1)}, u32[]{:S(2)}) copy-start(f32[512]{0:T(512)S(1)} %broadcast_multiply_fusion.3) | copy-start | bytes 6148
  231.9 19.7 %copy-start.48 = (f32[768]{0:T(1024)S(1)}, f32[768]{0:T(1024)}, u32[]{:S(2)}) copy-start(f32[768]{0:T(1024)} %convert_element_type.176) | copy-start | bytes 9220
  296.4 160.9 %reduce-scatter.5.cloned.1.call-start = ((), (), s32[]{:S(2)}) async-start(), calls=%async_computation.12 | async-start | bytes 7520256 | tf_op jit(solution)/shard_map/reduce_scatter | solution.py:255
  326.8 245.6 %reduce-scatter.11.cloned.1.call-start = ((), (), s32[]{:S(2)}) async-start(), calls=%async_computation.15 | async-start | bytes 10027008 | tf_op jit(solution)/shard_map/reduce_scatter | solution.py:263
  335.3 352.0 %reduce-scatter.9.cloned.1.call-start = ((), (), s32[]{:S(2)}) async-start(), calls=%async_computation.14 | async-start | bytes 10027008 | tf_op jit(solution)/shard_map/reduce_scatter | solution.py:261
  348.9 340.5 %copy-start.75 = (s32[1,16]{1,0:T(1,128)S(1)}, s32[1,16]{1,0:T(1,128)}, u32[]{:S(2)}) copy-start(s32[1,16]{1,0:T(1,128)} %param.35) | copy-start | bytes 196
  348.9 342.6 %copy-start.17 = (bf16[512,12,64]{0,2,1:T(8,128)(2,1)S(1)}, bf16[512,12,64]{0,2,1:T(8,128)(2,1)}, u32[]{:S(2)}) copy-start(bf16[512,12,64]{0,2,1:T(8,128)(2,1)} %copy-done.15) | copy-start | bytes 2359300
  348.9 344.1 %copy-start.45 = (f32[768]{0:T(1024)S(1)}, f32[768]{0:T(1024)}, u32[]{:S(2)}) copy-start(f32[768]{0:T(1024)} %get-tuple-element.17) | copy-start | bytes 9220
  348.9 344.1 %copy-start.46 = (f32[768]{0:T(1024)S(1)}, f32[768]{0:T(1024)}, u32[]{:S(2)}) copy-start(f32[768]{0:T(1024)} %get-tuple-element.48) | copy-start | bytes 9220
  348.9 344.1 %copy-start.51 = (f32[3072]{0:T(1024)S(1)}, f32[3072]{0:T(1024)}, u32[]{:S(2)}) copy-start(f32[3072]{0:T(1024)} %get-tuple-element.50) | copy-start | bytes 36868
  348.9 344.1 %copy-start.60 = (f32[768]{0:T(1024)S(1)}, f32[768]{0:T(1024)}, u32[]{:S(2)}) copy-start(f32[768]{0:T(1024)} %get-tuple-element.15) | copy-start | bytes 9220
  348.9 344.1 %copy-start.61 = (f32[768]{0:T(1024)S(1)}, f32[768]{0:T(1024)}, u32[]{:S(2)}) copy-start(f32[768]{0:T(1024)} %get-tuple-element.19) | copy-start | bytes 9220
  375.8 384.4 %all-to-all-start.1 = ((bf16[16,32,768]{2,1,0:T(8,128)(2,1)}), bf16[16,32,768]{2,1,0:T(8,128)(2,1)S(1)}, u32[]{:S(2)}, u32[]{:S(2)}) async-start(bf16[16,32,768]{2,1,0:T(8,128)(2,1)} %bitcast.189), calls=%async_computation.1 | async-start | bytes 1572864 | tf_op jit(solution)/shard_map/all_to_all | solution.py:302
  379.9 382.3 %all-reduce.22.cloned.1.call-start = ((), (), s32[]{:S(2)}) async-start(), calls=%async_computation.16 | async-start | bytes 3538944 | tf_op jit(solution)/shard_map/psum | solution.py:282
  (61 other events, 313.0 us)
Sparse Core Ops, SparseCore 0:
  10.3 60.6 all-gather.4
  73.3 41.1 all-gather.6
  116.8 62.7 all-gather.8
  181.7 60.6 all-gather.10
  296.6 67.6 reduce-scatter.6
  368.1 89.2 reduce-scatter.4
  461.5 110.8 reduce-scatter.10
  576.5 110.8 reduce-scatter.8
  689.9 55.5 all-reduce.21
